TPU v7x, 32 devices: a whole 2x2x4 slice. The times are simulated.
32 devices in a mesh: ep: 4 (over y, x), tp: 8 (over z, core).
Axes of the slice: x: 2, y: 2, z: 4, core: 2. Of those that a mesh axis runs over, the one named last changes fastest.
Arguments:
- tokens: bfloat16 [512, 6144], P('ep'), may hold values from -6 to 6
- expert_ids: int32 [512, 2], P('ep'), may hold values from 0 to 3, all different within a row; in each aligned block of 128 rows (0 to 127, 128 to 255, ...) at most 96 rows name the same one
- router: bfloat16 [6144, 4], replicated, may hold values from -0.078125 to 0.078125
- gate_weight: bfloat16 [4, 6144, 8192], P('ep', None, 'tp'), may hold values from -0.078125 to 0.078125
- up_weight: bfloat16 [4, 6144, 8192], P('ep', None, 'tp'), may hold values from -0.078125 to 0.078125
- down_weight: bfloat16 [4, 8192, 6144], P('ep', 'tp'), may hold values from -0.0625 to 0.0625
- keep_mask: int32 [512, 6144], P('ep'), may hold values 0 or 1
Outputs:
- layer_out: bfloat16 [512, 6144], P('ep')
Inputs may be any that keep to these rules, and one draw needn't show every extreme that they name: `expert_ids`: each row names two different experts. In the rows of one token block of 128 rows no expert is named more than 96 times, a bound that some block reaches.
All inputs are finite; a program needn't handle non-finite values. No bound on the sum of `keep_mask` on one device may be relied on, other than what follows from the above.
Results may differ from a plain program's by a relative error of at most 0.018.
Values may be sent and summed in bfloat16 or wider, within the bound.
A program may use at most 128 MiB of HBM per device.

v0:
```python
import jax
import jax.numpy as jnp
from jax import lax
from jax.sharding import PartitionSpec as P


def shards(tokens, expert_ids, router, gate_weight, up_weight, down_weight, keep_mask):
    experts = router.shape[1]
    tok_rows = tokens.shape[0]
    width_model = tokens.shape[1]
    capacity = 3 * tok_rows // experts
    groups = lax.axis_size("tp")
    share = capacity // groups
    logits = jnp.dot(tokens, router, preferred_element_type=jnp.float32)
    picked = jnp.take_along_axis(logits, expert_ids, axis=1)
    weight_first = jax.nn.sigmoid(picked[:, 0] - picked[:, 1])
    weight_second = jax.nn.sigmoid(picked[:, 1] - picked[:, 0])
    onehot = (expert_ids[:, :, None] == jnp.arange(experts, dtype=jnp.int32)[None, None, :]).astype(
        jnp.int32
    )
    onehot = onehot.reshape(tok_rows * 2, experts)
    ranks = jnp.cumsum(onehot, axis=0) - onehot
    slot = jnp.sum(ranks * onehot, axis=1).reshape(tok_rows, 2)
    place = slot * experts + expert_ids
    lines = jnp.arange(experts * capacity, dtype=jnp.int32)
    picker = ((place[None, :, 0] == lines[:, None]) | (place[None, :, 1] == lines[:, None])).astype(
        jnp.bfloat16
    )
    outgoing = jnp.dot(picker, tokens, preferred_element_type=jnp.float32).astype(jnp.bfloat16)
    outgoing = outgoing.reshape(capacity, experts, width_model)
    w_gate = gate_weight[0]
    w_up = up_weight[0]
    w_down = down_weight[0]
    arrived = lax.all_to_all(outgoing, "ep", split_axis=1, concat_axis=1, tiled=True)
    rows = arrived.reshape(capacity * experts, width_model)
    gate = jnp.dot(rows, w_gate, preferred_element_type=jnp.float32)
    up = jnp.dot(rows, w_up, preferred_element_type=jnp.float32)
    hidden = (jax.nn.silu(gate) * up).astype(jnp.bfloat16)
    summed = lax.psum_scatter(
        jnp.dot(hidden, w_down, preferred_element_type=jnp.float32).astype(jnp.bfloat16),
        "tp",
        scatter_dimension=0,
        tiled=True,
    )
    expert_out = summed.reshape(share, experts, width_model)
    back = lax.all_to_all(expert_out, "ep", split_axis=1, concat_axis=1, tiled=True)
    returned = lax.all_gather(back, "tp", axis=0, tiled=True)
    returned = returned.reshape(capacity * experts, width_model)
    first_rows = jnp.take(returned, place[:, 0], axis=0).astype(jnp.float32)
    second_rows = jnp.take(returned, place[:, 1], axis=0).astype(jnp.float32)
    combined = weight_first[:, None] * first_rows + weight_second[:, None] * second_rows
    return (combined * keep_mask.astype(jnp.float32) * 1.25).astype(jnp.bfloat16)


def solution(mesh):
    return jax.shard_map(
        shards,
        mesh=mesh,
        in_specs=(
            P("ep", None),
            P("ep", None),
            P(),
            P("ep", None, "tp"),
            P("ep", None, "tp"),
            P("ep", "tp", None),
            P("ep", None),
        ),
        out_specs=P("ep", None),
        check_vma=False,
    )
```

profile of v0, /device:TPU:0, one launch (start us, length us, event | category | flops | bytes accessed | tf_op | source)
XLA Modules:
  0.0 282.0 jit_solution(14242153663635588185)
XLA Ops:
  6.5 0.9 copy.59
  7.4 0.1 eq.60
  7.6 0.1 eq.56
  7.7 1.2 reduce-window.6
  9.0 0.1 copy.61
  9.2 0.1 copy.62
  9.4 0.1 mul.50
  9.6 0.2 slice_reduce_fusion.1
  9.8 0.6 copy-done.2
  10.3 3.5 %convolution_convert_fusion = bf16[384,6144]{1,0:T(8,128)(2,1)} fusion(bf16[128,6144]{1,0:T(8,128)(2,1)S(1)} %copy-done, s32[128]{0:T(128)S(1)} %get-tuple-element.7, s32[128]{0:T(128)S(1)} %get-tuple-element.6), kind=kOutput, calls=%fused_computation.10 | convolution fusion | flops 606486528 | bytes 6292480 | tf_op jit(solution)/shard_map/dot_general | solution.py:29
  13.8 7.6 %reshape.51 = bf16[96,4,6144]{2,1,0:T(4,128)(2,1)} reshape(bf16[384,6144]{1,0:T(8,128)(2,1)} %convolution_convert_fusion) | data formatting | bytes 9437184 | tf_op jit(solution)/shard_map/reshape | solution.py:30
  21.4 4.9 %copy.64 = bf16[96,4,6144]{2,0,1:T(8,128)(2,1)S(1)} copy(bf16[96,4,6144]{2,1,0:T(4,128)(2,1)} %reshape.51) | data formatting | bytes 9437184 | tf_op jit(solution)/shard_map/reshape | solution.py:30
  26.3 58.5 %all_to_all.10 = bf16[96,4,6144]{2,0,1:T(8,128)(2,1)S(1)} all-to-all(bf16[96,4,6144]{2,0,1:T(8,128)(2,1)S(1)} %copy.64), channel_id=1, replica_groups=mesh['ep'=4,'tp'=8] {'ep'}, dimensions={1} | all-to-all | bytes 9437184 | tf_op jit(solution)/shard_map/all_to_all | solution.py:34
  84.8 5.8 %copy.65 = bf16[96,4,6144]{2,1,0:T(4,128)(2,1)} copy(bf16[96,4,6144]{2,0,1:T(8,128)(2,1)S(1)} %all_to_all.10) | data formatting | bytes 9437184 | tf_op jit(solution)/shard_map/all_to_all | solution.py:34
  90.6 7.2 %reshape.52 = bf16[384,6144]{1,0:T(8,128)(2,1)} reshape(bf16[96,4,6144]{2,1,0:T(4,128)(2,1)} %copy.65) | data formatting | bytes 9437184 | tf_op jit(solution)/shard_map/reshape | solution.py:35
  97.8 9.6 %fusion.4 = f32[384,1024]{1,0:T(8,128)S(1)} fusion(bf16[384,6144]{1,0:T(8,128)(2,1)} %reshape.52, bf16[1,6144,1024]{2,1,0:T(8,128)(2,1)} %param.12), kind=kOutput, calls=%fused_computation.7 | convolution fusion | flops 4831838208 | bytes 18874368 | tf_op jit(solution)/shard_map/dot_general | solution.py:36
  107.3 21.7 %fusion.6 = bf16[384,6144]{1,0:T(8,128)(2,1)} fusion(bf16[1,1024,6144]{2,1,0:T(8,128)(2,1)} %param.14, f32[384,1024]{1,0:T(8,128)S(1)} %fusion.4, bf16[384,6144]{1,0:T(8,128)(2,1)} %reshape.52, bf16[1,6144,1024]{2,1,0:T(8,128)(2,1)} %param.13), kind=kOutput, calls=%fused_computation.9 | convolution fusion | flops 9668395008 | bytes 36175872 | tf_op jit(solution)/shard_map/dot_general | solution.py:40
  129.1 54.7 %reduce-scatter.2.cloned.1.call-done = bf16[48,6144]{1,0:T(8,128)(2,1)} async-done(((bf16[384,6144]{1,0:T(8,128)(2,1)}), bf16[48,6144]{1,0:T(8,128)(2,1)}) %reduce-scatter.2.cloned.1.call-update) | async-done | bytes 589840 | tf_op jit(solution)/shard_map/reduce_scatter | solution.py:39
  183.8 1.3 reshape.53
  185.1 0.3 copy.66
  185.4 12.9 %all_to_all.11 = bf16[12,4,6144]{2,0,1:T(8,128)(2,1)S(1)} all-to-all(bf16[12,4,6144]{2,0,1:T(8,128)(2,1)S(1)} %copy.66), channel_id=1, replica_groups=mesh['ep'=4,'tp'=8] {'ep'}, dimensions={1} | all-to-all | bytes 1179648 | tf_op jit(solution)/shard_map/all_to_all | solution.py:46
  198.3 1.3 copy.67
  199.6 0.1 copy.57
  199.7 0.1 reshape.71
  199.9 0.5 fusion.22
  200.4 2.4 gather_fusion
  202.8 0.1 reshape.74
  203.1 46.7 %all-gather.2.cloned.1.call-done = bf16[96,4,6144]{2,1,0:T(4,128)(2,1)} async-done(((bf16[12,4,6144]{2,1,0:T(4,128)(2,1)}), bf16[96,4,6144]{2,1,0:T(4,128)(2,1)}) %all-gather.2.cloned.1.call-update) | async-done | bytes 4718608 | tf_op jit(solution)/shard_map/all_gather | solution.py:47
  249.9 7.2 %reshape.54 = bf16[384,6144]{1,0:T(8,128)(2,1)} reshape(bf16[96,4,6144]{2,1,0:T(4,128)(2,1)} %all-gather.2.cloned.1.call-done) | data formatting | bytes 9437184 | tf_op jit(solution)/shard_map/reshape | solution.py:48
  257.1 5.9 %gather_fusion.1 = bf16[128,6144]{1,0:T(8,128)(2,1)S(1)} fusion(bf16[384,6144]{1,0:T(8,128)(2,1)} %reshape.54, s32[1024]{0:T(1024)S(1)} %pad_clamp_fusion.1), kind=kCustom, calls=%fused_computation.clone | custom fusion | bytes 3146240 | tf_op jit(solution)/shard_map/jit(_take)/gather | solution.py:49
  263.1 7.1 %gather_fusion.2 = bf16[128,6144]{1,0:T(8,128)(2,1)} fusion(bf16[384,6144]{1,0:T(8,128)(2,1)} %reshape.54, s32[1024]{0:T(1024)S(1)} %pad_clamp_fusion), kind=kCustom, calls=%fused_computation.1.clone | custom fusion | bytes 3146240 | tf_op jit(solution)/shard_map/jit(_take)/gather | solution.py:50
  270.2 5.0 %multiply_convert_fusion = bf16[128,6144]{1,0:T(8,128)(2,1)} fusion(s32[128,6144]{1,0:T(8,128)} %param.15, bf16[128,6144]{1,0:T(8,128)(2,1)} %gather_fusion.2, bf16[128,6144]{1,0:T(8,128)(2,1)S(1)} %gather_fusion.1, f32[128]{0:T(128)S(1)} %get-tuple-element.9, f32[128]{0:T(128)S(1)} %get-tuple-element.8, pred[128]{0:T(512)(128)(4,1)S(1)} %get-tuple-element.12, ...), kind=kLoop, calls=%fused_computation.11 | loop fusion | flops 8650752 | bytes 7865600 | tf_op jit(solution)/shard_map/convert_element_type | solution.py:52
  (33 shorter events, 0.5 us)
Async XLA Ops:
  6.5 3.8 %copy-start = (bf16[128,6144]{1,0:T(8,128)(2,1)S(1)}, bf16[128,6144]{1,0:T(8,128)(2,1)}, u32[]{:S(2)}) copy-start(bf16[128,6144]{1,0:T(8,128)(2,1)} %param.9) | copy-start | bytes 4718596
  6.5 177.2 %reduce-scatter.2.cloned.1.call-start = ((), (), s32[]{:S(2)}) async-start(), calls=%async_computation.3 | async-start | bytes 5308416 | tf_op jit(solution)/shard_map/reduce_scatter | solution.py:39
  9.7 0.6 copy-start.2
  9.7 0.6 copy-start.4
  129.0 70.6 %copy-start.6 = (s32[128,2]{0,1:T(2,128)S(1)}, s32[128,2]{0,1:T(2,128)}, u32[]{:S(2)}) copy-start(s32[128,2]{0,1:T(2,128)} %param.10) | copy-start | bytes 3076
  129.1 70.8 %copy-start.1 = (bf16[6144,4]{0,1:T(4,128)(2,1)S(1)}, bf16[6144,4]{0,1:T(4,128)(2,1)}, u32[]{:S(2)}) copy-start(bf16[6144,4]{0,1:T(4,128)(2,1)} %param.11) | copy-start | bytes 147460
  129.1 120.8 %all-gather.2.cloned.1.call-start = ((), (), s32[]{:S(2)}) async-start(), calls=%async_computation.4 | async-start | bytes 5308416 | tf_op jit(solution)/shard_map/all_gather | solution.py:47
  200.4 2.6 copy-start.3
  200.4 2.6 copy-start.5
Sparse Core Ops, SparseCore 0:
  129.2 54.5 reduce-scatter.1
  199.7 50.0 all-gather.1
where the time goes:
time: 283 us; the launch traced here: 282 us
  waiting for transfers between devices  101 us (36%)
  blocking collectives  71.4 us (25%)
  local copies, waits for them, and re-layouts  53.9 us (19%)
  matrix products  35.2 us (12%)
  between operations  13.6 us (5%)
  other arithmetic  6.43 us (2%)
    all_to_all x1, blocking collectives, shards(): lax.all_to_all(outgoing, 'ep', split_axis=1, concat_axis=1, tiled=True)  58.5 us
    reduce_scatter x1, waiting for transfers between devices, shards(): lax.psum_scatter(jnp.dot(hidden, w_down, preferred_element_type=jnp.float...  54.7 us
    all_gather x1, waiting for transfers between devices, shards(): returned = lax.all_gather(back, 'tp', axis=0, tiled=True)  46.7 us
    dot_general x1, matrix products, shards(): jnp.dot(hidden, w_down, preferred_element_type=jnp.float32)  21.7 us
    all_to_all x1, blocking collectives, shards(): lax.all_to_all(expert_out, 'ep', split_axis=1, concat_axis=1, tiled=True)  12.9 us
    reshape x2, local copies, waits for them, and re-layouts, shards(): outgoing = outgoing.reshape(capacity, experts, width_model)  12.5 us
    dot_general x1, matrix products, shards(): gate = jnp.dot(rows, w_gate, preferred_element_type=jnp.float32)  9.55 us
    reshape x1, local copies, waits for them, and re-layouts, shards(): returned = returned.reshape(capacity * experts, width_model)  7.25 us
  transfers between devices with their start and end apart: 2, of which 2 were waited for; matrix products, arithmetic and copies ran while one was open for 1% of the time, Pallas kernels for 0%

commit v1 on v0

v1 whole, which is shorter than its diff:
```python
import functools

import jax
import jax.numpy as jnp
from jax import lax
from jax.experimental import pallas as pl
from jax.experimental.pallas import tpu as pltpu
from jax.sharding import PartitionSpec as P

MESH = pl.DeviceIdType.MESH


def flip(index, offset, count):
    out, bit = 0, 1
    while bit < count:
        out = out + ((index // bit + offset // bit) % 2) * bit
        bit *= 2
    return out


def kernel(
    n_ep, nz, slots_ref, comb_ref, gate_hbm, up_hbm, down_hbm, mask_hbm, out_ref,
    w_gate, w_up, w_down, mask, rows, hidden, pair_out, pair_in, mine, ep_out, ep_in,
    z_out, z_in, local_sem, disp_s, disp_r, fwd_s, fwd_r, pair_s, pair_r, ep_s, ep_r,
    z_s, z_r, gat_s, gat_r, gfw_s, gfw_r,
):
    ep, tp = lax.axis_index("ep"), lax.axis_index("tp")
    z, core = tp // 2, tp % 2
    partner = (ep, z * 2 + (1 - core))
    cap, width = rows.shape[1], rows.shape[2]
    toks = out_ref.shape[0]
    ff = w_gate.shape[1]
    half, piece = width // 2, width // (2 * nz)
    total_rows = n_ep * cap

    def cols(owner_core, owner_z):
        return pl.ds(pl.multiple_of((owner_core * nz + owner_z) * piece, 128), piece)

    my_half = pl.ds(pl.multiple_of(core * half, 128), half)

    load_own = pltpu.make_async_copy(slots_ref.at[ep], rows.at[0], local_sem.at[0])
    load_gate = pltpu.make_async_copy(gate_hbm, w_gate, local_sem.at[1])
    load_up = pltpu.make_async_copy(up_hbm, w_up, local_sem.at[2])
    load_down = pltpu.make_async_copy(down_hbm, w_down, local_sem.at[3])
    load_mask = pltpu.make_async_copy(mask_hbm.at[:, cols(core, z)], mask, local_sem.at[4])
    for load in (load_own, load_gate, load_up):
        load.start()

    barrier = pltpu.get_barrier_semaphore()
    peers = [(flip(ep, o, n_ep), tp) for o in range(1, n_ep)]
    peers += [(ep, ((z + s) % nz) * 2 + core) for s in range(1, nz)] + [partner]
    for peer in peers:
        pl.semaphore_signal(barrier, inc=1, device_id=peer, device_id_type=MESH)
    pl.semaphore_wait(barrier, len(peers))

    def remote(src, dst, send, recv, device):
        return pltpu.make_async_remote_copy(
            src_ref=src, dst_ref=dst, send_sem=send, recv_sem=recv,
            device_id=device, device_id_type=MESH,
        )

    started = []

    dispatch = [None]
    for o in range(1, n_ep):
        peer = flip(ep, o, n_ep)
        copy = remote(slots_ref.at[peer, :, my_half], rows.at[o, :, my_half],
                      disp_s.at[o], disp_r.at[o], (peer, tp))
        copy.start()
        dispatch.append(copy)
        started.append(copy)
    load_down.start()
    load_mask.start()

    forward = [None]
    for o in range(1, n_ep):
        forward.append(remote(rows.at[o, :, my_half], rows.at[o, :, my_half],
                              fwd_s.at[o], fwd_r.at[o], partner))

    tile = min(256, ff)
    phases = 2
    per = n_ep // phases
    for phase in range(phases):
        for o in range(phase * per, (phase + 1) * per):
            if o > 0:
                dispatch[o].wait_recv()
                forward[o].start()
                started.append(forward[o])
        if phase == 0:
            load_own.wait()
            load_gate.wait()
            load_up.wait()
        for o in range(phase * per, (phase + 1) * per):
            if o > 0:
                forward[o].wait_recv()

        def up_step(t, carry):
            at = pl.ds(pl.multiple_of(t * tile, tile), tile)
            block = rows[phase * per:(phase + 1) * per].reshape(per * cap, width)
            gate = jnp.dot(block, w_gate[:, at], preferred_element_type=jnp.float32)
            up = jnp.dot(block, w_up[:, at], preferred_element_type=jnp.float32)
            hidden[phase * per * cap:(phase + 1) * per * cap, at] = (
                jax.nn.silu(gate) * up).astype(jnp.bfloat16)
            return carry

        lax.fori_loop(0, ff // tile, up_step, 0)

    load_down.wait()

    def pair_sum(s):
        pair[s].wait_recv()
        summed = (mine[s % 2].astype(jnp.float32) + pair_in[s].astype(jnp.float32)).astype(jnp.bfloat16)
        ep_in[s, 0:cap, :] = summed[0:cap]
        ep_out[s] = summed[cap:]
        for o in range(1, n_ep):
            copy = remote(ep_out.at[s, pl.ds((o - 1) * cap, cap), :], ep_in.at[s, pl.ds(o * cap, cap), :],
                          ep_s.at[s, o], ep_r.at[s, o], (flip(ep, o, n_ep), tp))
            copy.start()
            exchange[s].append(copy)
            started.append(copy)

    pair, exchange = [], [[] for _ in range(nz)]
    for s in range(nz):
        owner = (z + 1 + s) % nz
        pair_out[s] = jnp.dot(hidden[...], w_down[:, cols(1 - core, owner)],
                              preferred_element_type=jnp.float32).astype(jnp.bfloat16)
        copy = remote(pair_out.at[s], pair_in.at[s], pair_s.at[s], pair_r.at[s], partner)
        copy.start()
        pair.append(copy)
        started.append(copy)
        mine[s % 2] = jnp.dot(hidden[...], w_down[:, cols(core, owner)],
                              preferred_element_type=jnp.float32).astype(jnp.bfloat16)
        pair_sum(s)

    reduce = []
    for s in range(nz):
        owner = (z + 1 + s) % nz
        for copy in exchange[s]:
            copy.wait_recv()
        both = jnp.dot(comb_ref[...], ep_in[s], preferred_element_type=jnp.float32)
        token_sum = both[0:toks] + both[toks:]
        if s < nz - 1:
            z_out[s] = token_sum.astype(jnp.bfloat16)
            copy = remote(z_out.at[s], z_in.at[s], z_s.at[s], z_r.at[s], (ep, owner * 2 + core))
            copy.start()
            reduce.append(copy)
            started.append(copy)
    for s in range(nz - 1):
        reduce[s].wait_recv()
        token_sum = token_sum + z_in[s].astype(jnp.float32)
    load_mask.wait()
    out_ref[:, cols(core, z)] = (token_sum * mask[...].astype(jnp.float32) * 1.25).astype(jnp.bfloat16)

    gather = []
    here = out_ref.at[:, cols(core, z)]
    for s in range(1, nz):
        copy = remote(here, here, gat_s.at[s], gat_r.at[s], (ep, ((z + s) % nz) * 2 + core))
        copy.start()
        gather.append(copy)
        started.append(copy)
    passed = [remote(here, here, gfw_s.at[0], gfw_r.at[0], partner)]
    passed[0].start()
    started.append(passed[0])
    for s in range(1, nz):
        gather[s - 1].wait_recv()
        there = out_ref.at[:, cols(core, (z + nz - s) % nz)]
        copy = remote(there, there, gfw_s.at[s], gfw_r.at[s], partner)
        copy.start()
        passed.append(copy)
        started.append(copy)
    for copy in passed:
        copy.wait_recv()
    for copy in started:
        copy.wait_send()


def shards(n_ep, n_tp, tokens, expert_ids, router, gate_weight, up_weight, down_weight, keep_mask):
    experts = router.shape[1]
    toks, width = tokens.shape
    cap = 3 * toks // experts
    nz = n_tp // 2
    piece = width // n_tp
    total = experts * cap
    logits = jnp.dot(tokens, router, preferred_element_type=jnp.float32)
    numbers = jnp.arange(experts, dtype=jnp.int32)
    onehot3 = expert_ids[:, :, None] == numbers[None, None, :]
    picked = jnp.sum(jnp.where(onehot3, logits[:, None, :], 0.0), axis=2)
    weight_first = jax.nn.sigmoid(picked[:, 0] - picked[:, 1])
    weight_second = jax.nn.sigmoid(picked[:, 1] - picked[:, 0])
    onehot = onehot3.astype(jnp.float32)
    named = onehot[:, 0] + onehot[:, 1]
    order = jnp.arange(toks, dtype=jnp.int32)
    before = (order[None, :] < order[:, None]).astype(jnp.bfloat16)
    ranks = jnp.dot(before, named.astype(jnp.bfloat16), preferred_element_type=jnp.float32)
    slot = jnp.sum(ranks[:, None, :] * onehot, axis=2).astype(jnp.int32)
    lines = jnp.arange(total, dtype=jnp.int32)
    place = expert_ids * cap + slot
    picker = ((place[None, :, 0] == lines[:, None]) | (place[None, :, 1] == lines[:, None])).astype(jnp.bfloat16)
    slots = jnp.dot(picker, tokens, preferred_element_type=jnp.float32).astype(jnp.bfloat16)
    slots = slots.reshape(experts, cap, width)
    turned = jnp.bitwise_xor(expert_ids, lax.axis_index("ep")) * cap + slot
    comb = (jnp.where(turned[:, 0:1] == lines[None, :], weight_first[:, None], 0.0)
            + jnp.where(turned[:, 1:2] == lines[None, :], weight_second[:, None], 0.0))
    high = lax.reduce_precision(comb, 8, 7)
    comb = jnp.concatenate([high, comb - high], axis=0).astype(jnp.bfloat16)
    w_gate, w_up, w_down = gate_weight[0], up_weight[0], down_weight[0]
    ff = w_gate.shape[1]
    vmem, hbm = pl.BlockSpec(memory_space=pltpu.VMEM), pl.BlockSpec(memory_space=pl.ANY)
    bf = jnp.bfloat16
    dma = pltpu.SemaphoreType.DMA
    return pl.pallas_call(
        functools.partial(kernel, n_ep, nz),
        out_shape=jax.ShapeDtypeStruct((toks, width), bf),
        in_specs=[vmem, vmem, hbm, hbm, hbm, hbm],
        out_specs=vmem,
        scratch_shapes=[
            pltpu.VMEM((width, ff), bf), pltpu.VMEM((width, ff), bf), pltpu.VMEM((ff, width), bf),
            pltpu.VMEM((toks, piece), jnp.int32),
            pltpu.VMEM((experts, cap, width), bf),
            pltpu.VMEM((total, ff), bf),
            pltpu.VMEM((nz, total, piece), bf), pltpu.VMEM((nz, total, piece), bf),
            pltpu.VMEM((2, total, piece), bf),
            pltpu.VMEM((nz, total - cap, piece), bf), pltpu.VMEM((nz, total, piece), bf),
            pltpu.VMEM((nz - 1, toks, piece), bf), pltpu.VMEM((nz - 1, toks, piece), bf),
            dma((5,)), dma((n_ep,)), dma((n_ep,)), dma((n_ep,)), dma((n_ep,)),
            dma((nz,)), dma((nz,)), dma((nz, n_ep)), dma((nz, n_ep)),
            dma((nz,)), dma((nz,)), dma((nz,)), dma((nz,)), dma((nz,)), dma((nz,)),
        ],
        compiler_params=pltpu.CompilerParams(
            collective_id=0, has_side_effects=True, vmem_limit_bytes=67043328),
    )(slots, comb, w_gate, w_up, w_down, keep_mask)


def solution(mesh):
    return jax.shard_map(
        functools.partial(shards, mesh.shape["ep"], mesh.shape["tp"]),
        mesh=mesh,
        in_specs=(
            P("ep", None),
            P("ep", None),
            P(),
            P("ep", None, "tp"),
            P("ep", None, "tp"),
            P("ep", "tp", None),
            P("ep", None),
        ),
        out_specs=P("ep", None),
        check_vma=False,
    )
```

time: 283 us -> 107 us (0.38)
  the two profiles are of different devices: /device:TPU:0 before, /device:TPU:31 now
where the time goes in v1:
time: 107 us
  Pallas kernels  97.2 us (91%)
  matrix products  5.66 us (5%)
  local copies, waits for them, and re-layouts  2.7 us (3%)
    pallas_call x1, Pallas kernels, shards(): pl.pallas_call(functools.partial(kernel, n_ep, nz), out_shape=jax.ShapeDt...  97.2 us
    dot_general x1, matrix products, shards(): jnp.dot(picker, tokens, preferred_element_type=jnp.float32)  3.49 us
    unnamed x5, local copies, waits for them, and re-layouts  2.7 us

profile of v1, /device:TPU:31, one launch (start us, length us, event | category | flops | bytes accessed | tf_op | source)
XLA Modules:
  0.0 106.5 jit_solution(18104620413072891847)
XLA Ops:
  0.0 0.0 copy-start.1
  0.0 0.0 copy-start
  0.0 2.0 %fusion.10 = f32[128,4]{0,1:T(4,128)S(1)} fusion(bf16[128,6144]{1,0:T(8,128)(2,1)} %param.7, bf16[6144,4]{0,1:T(4,128)(2,1)} %param.9), kind=kOutput, calls=%fused_computation.30 | convolution fusion | flops 6291456 | bytes 1624064 | tf_op jit(solution)/shard_map/dot_general | solution.py:184
  2.0 0.0 copy-done.1
  2.1 0.1 fusion.5
  2.3 0.1 reduce-precision_convert_fusion
  2.4 0.7 pad_maximum_fusion.comb_ref
  3.1 0.0 copy-done
  3.1 3.5 %convolution_convert_fusion = bf16[384,6144]{1,0:T(8,128)(2,1)} fusion(bf16[128,6144]{1,0:T(8,128)(2,1)S(1)} %copy-done, s32[128]{0:T(128)S(1)} %get-tuple-element.17, s32[128]{0:T(128)S(1)} %get-tuple-element.18), kind=kOutput, calls=%fused_computation | convolution fusion | flops 606486528 | bytes 6292480 | tf_op jit(solution)/shard_map/dot_general | solution.py:199
  6.6 97.2 %shard_map.73 = bf16[128,6144]{1,0:T(8,128)(2,1)} custom-call(bf16[4,96,6144]{2,1,0:T(8,128)(2,1)} %bitcast.22, bf16[256,384]{1,0:T(8,128)(2,1)} %pad_maximum_fusion.comb_ref, bf16[6144,1024]{1,0:T(8,128)(2,1)} %bitcast.23, bf16[6144,1024]{1,0:T(8,128)(2,1)} %bitcast.24, bf16[1024,6144]{1,0:T(8,128)(2,1)} %bitcast.25, s32[128,6144]{1,0:T(8,128)} %mask_hbm.1), custom_call_target="tpu_custom_call" | custom-call | tf_op jit(solution)/shard_map/pallas_call | solution.py:211
  103.9 2.7 %copy.12 = bf16[128,6144]{1,0:T(8,128)(2,1)} copy(bf16[128,6144]{1,0:T(8,128)(2,1)} %shard_map.73) | data formatting | bytes 3145728
  (5 shorter events, 0.1 us)
Async XLA Ops:
  0.0 2.0 %copy-start.1 = (s32[128,2]{0,1:T(2,128)S(1)}, s32[128,2]{0,1:T(2,128)}, u32[]{:S(2)}) copy-start(s32[128,2]{0,1:T(2,128)} %param.8) | copy-start | bytes 3076
  0.0 3.1 %copy-start = (bf16[128,6144]{1,0:T(8,128)(2,1)S(1)}, bf16[128,6144]{1,0:T(8,128)(2,1)}, u32[]{:S(2)}) copy-start(bf16[128,6144]{1,0:T(8,128)(2,1)} %param.7) | copy-start | bytes 4718596

commit v2 on v1

--- a/solution.py
+++ b/solution.py
@@ -33,8 +33,13 @@
     half, piece = width // 2, width // (2 * nz)
     total_rows = n_ep * cap
 
-    def cols(owner_core, owner_z):
-        return pl.ds(pl.multiple_of((owner_core * nz + owner_z) * piece, 128), piece)
+    rounds = pair_in.shape[0] // nz
+    sub = piece // rounds
+
+    def cols(owner_core, owner_z, turn=None):
+        if turn is None:
+            return pl.ds(pl.multiple_of((owner_core * nz + owner_z) * piece, 128), piece)
+        return pl.ds(pl.multiple_of((owner_core * nz + owner_z) * piece + turn * sub, 128), sub)
 
     my_half = pl.ds(pl.multiple_of(core * half, 128), half)
 
@@ -61,21 +66,47 @@
 
     started = []
 
-    dispatch = [None]
+    third = half // 3
+    odd = z % 2
+    z_pair = (ep, (z + 1 - 2 * odd) * 2 + core)
+
+    def part(which):
+        return pl.ds(pl.multiple_of(core * half + which * third, 128), third)
+
+    shared, common, foreign = part(2 * odd), part(1), part(2 - 2 * odd)
+    arrive, forward = {}, {}
+
+    def send_rows(o, kind, at):
+        peer = flip(ep, o, n_ep)
+        copy = remote(slots_ref.at[peer, :, at], rows.at[o, :, at],
+                      disp_s.at[kind, o], disp_r.at[kind, o], (peer, tp))
+        copy.start()
+        arrive[kind, o] = copy
+        started.append(copy)
+
+    def pass_on(o, kind, at):
+        arrive[kind, o].wait_recv()
+        if kind == 0:
+            copy = remote(rows.at[o, :, at], rows.at[o, :, at],
+                          disp_s.at[2, o], disp_r.at[2, o], z_pair)
+            copy.start()
+            arrive[2, o] = copy
+            started.append(copy)
+        copy = remote(rows.at[o, :, at], rows.at[o, :, at],
+                      fwd_s.at[kind, o], fwd_r.at[kind, o], partner)
+        copy.start()
+        forward[kind, o] = copy
+        started.append(copy)
+
+    share_order = [n_ep - 1] + list(range(1, n_ep - 1))
+    for o in share_order:
+        send_rows(o, 0, shared)
     for o in range(1, n_ep):
-        peer = flip(ep, o, n_ep)
-        copy = remote(slots_ref.at[peer, :, my_half], rows.at[o, :, my_half],
-                      disp_s.at[o], disp_r.at[o], (peer, tp))
-        copy.start()
-        dispatch.append(copy)
-        started.append(copy)
+        send_rows(o, 1, common)
     load_down.start()
     load_mask.start()
-
-    forward = [None]
-    for o in range(1, n_ep):
-        forward.append(remote(rows.at[o, :, my_half], rows.at[o, :, my_half],
-                              fwd_s.at[o], fwd_r.at[o], partner))
+    for o in share_order:
+        pass_on(o, 0, shared)
 
     tile = min(256, ff)
     phases = 2
@@ -83,16 +114,16 @@
     for phase in range(phases):
         for o in range(phase * per, (phase + 1) * per):
             if o > 0:
-                dispatch[o].wait_recv()
-                forward[o].start()
-                started.append(forward[o])
+                pass_on(o, 1, common)
+                pass_on(o, 2, foreign)
         if phase == 0:
             load_own.wait()
             load_gate.wait()
             load_up.wait()
         for o in range(phase * per, (phase + 1) * per):
             if o > 0:
-                forward[o].wait_recv()
+                for kind in range(3):
+                    forward[kind, o].wait_recv()
 
         def up_step(t, carry):
             at = pl.ds(pl.multiple_of(t * tile, tile), tile)
@@ -119,55 +150,68 @@
             exchange[s].append(copy)
             started.append(copy)
 
-    pair, exchange = [], [[] for _ in range(nz)]
-    for s in range(nz):
-        owner = (z + 1 + s) % nz
-        pair_out[s] = jnp.dot(hidden[...], w_down[:, cols(1 - core, owner)],
+    pair, exchange = [], [[] for _ in range(rounds * nz)]
+    for s in range(rounds * nz):
+        turn, owner = s // nz, (z + 1 + s % nz) % nz
+        pair_out[s] = jnp.dot(hidden[...], w_down[:, cols(1 - core, owner, turn)],
                               preferred_element_type=jnp.float32).astype(jnp.bfloat16)
         copy = remote(pair_out.at[s], pair_in.at[s], pair_s.at[s], pair_r.at[s], partner)
         copy.start()
         pair.append(copy)
         started.append(copy)
-        mine[s % 2] = jnp.dot(hidden[...], w_down[:, cols(core, owner)],
+        if s > 0:
+            pair_sum(s - 1)
+        mine[s % 2] = jnp.dot(hidden[...], w_down[:, cols(core, owner, turn)],
                               preferred_element_type=jnp.float32).astype(jnp.bfloat16)
-        pair_sum(s)
-
-    reduce = []
-    for s in range(nz):
-        owner = (z + 1 + s) % nz
-        for copy in exchange[s]:
-            copy.wait_recv()
-        both = jnp.dot(comb_ref[...], ep_in[s], preferred_element_type=jnp.float32)
-        token_sum = both[0:toks] + both[toks:]
-        if s < nz - 1:
-            z_out[s] = token_sum.astype(jnp.bfloat16)
-            copy = remote(z_out.at[s], z_in.at[s], z_s.at[s], z_r.at[s], (ep, owner * 2 + core))
-            copy.start()
-            reduce.append(copy)
-            started.append(copy)
-    for s in range(nz - 1):
-        reduce[s].wait_recv()
-        token_sum = token_sum + z_in[s].astype(jnp.float32)
+    pair_sum(rounds * nz - 1)
+
     load_mask.wait()
-    out_ref[:, cols(core, z)] = (token_sum * mask[...].astype(jnp.float32) * 1.25).astype(jnp.bfloat16)
-
-    gather = []
-    here = out_ref.at[:, cols(core, z)]
-    for s in range(1, nz):
-        copy = remote(here, here, gat_s.at[s], gat_r.at[s], (ep, ((z + s) % nz) * 2 + core))
-        copy.start()
-        gather.append(copy)
-        started.append(copy)
-    passed = [remote(here, here, gfw_s.at[0], gfw_r.at[0], partner)]
-    passed[0].start()
-    started.append(passed[0])
-    for s in range(1, nz):
-        gather[s - 1].wait_recv()
-        there = out_ref.at[:, cols(core, (z + nz - s) % nz)]
-        copy = remote(there, there, gfw_s.at[s], gfw_r.at[s], partner)
+    gather = {}
+    passed = []
+
+    def hand_over(turn):
+        for s in range(1, nz):
+            gather[turn, s].wait_recv()
+            there = out_ref.at[:, cols(core, (z + nz - s) % nz, turn)]
+            copy = remote(there, there, gfw_s.at[turn, s], gfw_r.at[turn, s], partner)
+            copy.start()
+            passed.append(copy)
+            started.append(copy)
+
+    for turn in range(rounds):
+        reduce = []
+        for s in range(nz):
+            step = turn * nz + s
+            owner = (z + 1 + s) % nz
+            for copy in exchange[step]:
+                copy.wait_recv()
+            both = jnp.dot(comb_ref[...], ep_in[step], preferred_element_type=jnp.float32)
+            token_sum = both[0:toks] + both[toks:]
+            if s < nz - 1:
+                z_out[turn, s] = token_sum.astype(jnp.bfloat16)
+                copy = remote(z_out.at[turn, s], z_in.at[turn, s], z_s.at[turn, s], z_r.at[turn, s],
+                              (ep, owner * 2 + core))
+                copy.start()
+                reduce.append(copy)
+                started.append(copy)
+        for s in range(nz - 1):
+            reduce[s].wait_recv()
+            token_sum = token_sum + z_in[turn, s].astype(jnp.float32)
+        keep = mask[:, turn * sub:(turn + 1) * sub].astype(jnp.float32)
+        out_ref[:, cols(core, z, turn)] = (token_sum * keep * 1.25).astype(jnp.bfloat16)
+        here = out_ref.at[:, cols(core, z, turn)]
+        for s in range(1, nz):
+            copy = remote(here, here, gat_s.at[turn, s], gat_r.at[turn, s], (ep, ((z + s) % nz) * 2 + core))
+            copy.start()
+            gather[turn, s] = copy
+            started.append(copy)
+        copy = remote(here, here, gfw_s.at[turn, 0], gfw_r.at[turn, 0], partner)
         copy.start()
         passed.append(copy)
         started.append(copy)
+        if turn > 0:
+            hand_over(turn - 1)
+    hand_over(rounds - 1)
     for copy in passed:
         copy.wait_recv()
     for copy in started:
@@ -181,6 +225,8 @@
     nz = n_tp // 2
     piece = width // n_tp
     total = experts * cap
+    rounds = 3 if piece % 384 == 0 and piece > 384 else 1
+    sub, steps = piece // rounds, rounds * nz
     logits = jnp.dot(tokens, router, preferred_element_type=jnp.float32)
     numbers = jnp.arange(experts, dtype=jnp.int32)
     onehot3 = expert_ids[:, :, None] == numbers[None, None, :]
@@ -218,13 +264,14 @@
             pltpu.VMEM((toks, piece), jnp.int32),
             pltpu.VMEM((experts, cap, width), bf),
             pltpu.VMEM((total, ff), bf),
-            pltpu.VMEM((nz, total, piece), bf), pltpu.VMEM((nz, total, piece), bf),
-            pltpu.VMEM((2, total, piece), bf),
-            pltpu.VMEM((nz, total - cap, piece), bf), pltpu.VMEM((nz, total, piece), bf),
-            pltpu.VMEM((nz - 1, toks, piece), bf), pltpu.VMEM((nz - 1, toks, piece), bf),
-            dma((5,)), dma((n_ep,)), dma((n_ep,)), dma((n_ep,)), dma((n_ep,)),
-            dma((nz,)), dma((nz,)), dma((nz, n_ep)), dma((nz, n_ep)),
-            dma((nz,)), dma((nz,)), dma((nz,)), dma((nz,)), dma((nz,)), dma((nz,)),
+            pltpu.VMEM((steps, total, sub), bf), pltpu.VMEM((steps, total, sub), bf),
+            pltpu.VMEM((2, total, sub), bf),
+            pltpu.VMEM((steps, total - cap, sub), bf), pltpu.VMEM((steps, total, sub), bf),
+            pltpu.VMEM((rounds, nz - 1, toks, sub), bf), pltpu.VMEM((rounds, nz - 1, toks, sub), bf),
+            dma((5,)), dma((3, n_ep)), dma((3, n_ep)), dma((3, n_ep)), dma((3, n_ep)),
+            dma((steps,)), dma((steps,)), dma((steps, n_ep)), dma((steps, n_ep)),
+            dma((rounds, nz)), dma((rounds, nz)), dma((rounds, nz)), dma((rounds, nz)),
+            dma((rounds, nz)), dma((rounds, nz)),
         ],
         compiler_params=pltpu.CompilerParams(
             collective_id=0, has_side_effects=True, vmem_limit_bytes=67043328),

time: 107 us -> 107 us (level)
  the two profiles are of different devices: /device:TPU:31 before, /device:TPU:0 now
where the time goes in v2:
time: 107 us; the launch traced here: 106 us
  Pallas kernels  97.1 us (91%)
  matrix products  5.65 us (5%)
  local copies, waits for them, and re-layouts  2.7 us (3%)
    pallas_call x1, Pallas kernels, shards(): pl.pallas_call(functools.partial(kernel, n_ep, nz), out_shape=jax.ShapeDt...  97.1 us
    dot_general x1, matrix products, shards(): jnp.dot(picker, tokens, preferred_element_type=jnp.float32)  3.49 us
    unnamed x5, local copies, waits for them, and re-layouts  2.7 us

profile of v2, /device:TPU:0, one launch (start us, length us, event | category | flops | bytes accessed | tf_op | source)
XLA Modules:
  0.0 106.4 jit_solution(5848736834375892069)
XLA Ops:
  0.0 0.0 copy-start.1
  0.0 0.0 copy-start
  0.0 2.0 %fusion.10 = f32[128,4]{0,1:T(4,128)S(1)} fusion(bf16[128,6144]{1,0:T(8,128)(2,1)} %param.7, bf16[6144,4]{0,1:T(4,128)(2,1)} %param.9), kind=kOutput, calls=%fused_computation.30 | convolution fusion | flops 6291456 | bytes 1624064 | tf_op jit(solution)/shard_map/dot_general | solution.py:230
  2.0 0.0 copy-done.1
  2.1 0.1 fusion.5
  2.3 0.1 reduce-precision_convert_fusion
  2.4 0.7 pad_maximum_fusion.comb_ref
  3.1 0.0 copy-done
  3.1 3.5 %convolution_convert_fusion = bf16[384,6144]{1,0:T(8,128)(2,1)} fusion(bf16[128,6144]{1,0:T(8,128)(2,1)S(1)} %copy-done, s32[128]{0:T(128)S(1)} %get-tuple-element.17, s32[128]{0:T(128)S(1)} %get-tuple-element.18), kind=kOutput, calls=%fused_computation | convolution fusion | flops 606486528 | bytes 6292480 | tf_op jit(solution)/shard_map/dot_general | solution.py:245
  6.6 97.1 %shard_map.73 = bf16[128,6144]{1,0:T(8,128)(2,1)} custom-call(bf16[4,96,6144]{2,1,0:T(8,128)(2,1)} %bitcast.22, bf16[256,384]{1,0:T(8,128)(2,1)} %pad_maximum_fusion.comb_ref, bf16[6144,1024]{1,0:T(8,128)(2,1)} %bitcast.23, bf16[6144,1024]{1,0:T(8,128)(2,1)} %bitcast.24, bf16[1024,6144]{1,0:T(8,128)(2,1)} %bitcast.25, s32[128,6144]{1,0:T(8,128)} %mask_hbm.1), custom_call_target="tpu_custom_call" | custom-call | tf_op jit(solution)/shard_map/pallas_call | solution.py:257
  103.8 2.7 %copy.12 = bf16[128,6144]{1,0:T(8,128)(2,1)} copy(bf16[128,6144]{1,0:T(8,128)(2,1)} %shard_map.73) | data formatting | bytes 3145728
  (5 shorter events, 0.1 us)
Async XLA Ops:
  0.0 2.0 %copy-start.1 = (s32[128,2]{0,1:T(2,128)S(1)}, s32[128,2]{0,1:T(2,128)}, u32[]{:S(2)}) copy-start(s32[128,2]{0,1:T(2,128)} %param.8) | copy-start | bytes 3076
  0.0 3.1 %copy-start = (bf16[128,6144]{1,0:T(8,128)(2,1)S(1)}, bf16[128,6144]{1,0:T(8,128)(2,1)}, u32[]{:S(2)}) copy-start(bf16[128,6144]{1,0:T(8,128)(2,1)} %param.7) | copy-start | bytes 4718596
